TPU v7x, 32 devices: a whole 2x2x4 slice. The times are simulated.
32 devices in a mesh: dp: 8 (over z, x), fsdp: 4 (over y, core).
Axes of the slice: x: 2, y: 2, z: 4, core: 2. Of those that a mesh axis runs over, the one named last changes fastest.
Arguments:
- patches: bfloat16 [8, 4, 192, 64], P('dp', 'fsdp'), may hold values from -6 to 6
- noise: bfloat16 [8, 4, 192, 64], P('dp', 'fsdp'), may hold values from -6 to 6
- bucket: int32 [8, 4], P(None, 'fsdp'), may hold values from 0 to 11
- tstep: int32 [8, 4], P('dp', 'fsdp'), may hold values from 0 to 999
- dest: int32 [8, 4], P(None, 'fsdp'), may hold values from 0 to 7, as said below
- embed_weight: bfloat16 [64, 2432], replicated, may hold values from -0.75 to 0.75
- gain: float32 [2432], replicated, may hold values from 0.1 to 1.9
- proj_weight: bfloat16 [2432, 1216], P('fsdp'), may hold values from -0.125 to 0.125
- cotangent: bfloat16 [8, 4, 2, 192, 1216], P('dp', 'fsdp'), may hold values from -6 to 6
Outputs:
- projected: bfloat16 [8, 4, 2, 192, 1216], P('dp', 'fsdp')
- embed_grad: float32 [64, 2432], replicated
Inputs may be any that keep to these rules, and one draw needn't show every extreme that they name: `dest`: in every column f, each dp index is named by at most 2 images and by exactly 2 for some.
All inputs are finite; a program needn't handle non-finite values.
Results may differ from a plain program's by a relative error of at most 0.006.
Values may be sent and summed in bfloat16 or wider, within the bound.
A program may use at most 64 MiB of HBM per device.

v0:
```python
import jax
import jax.numpy as jnp
from jax import lax
from jax.sharding import PartitionSpec as P

TOK_MAX = 192
CAP = 2
BUCKETS = 12
TSTEPS = 1000
norm_eps = 1e-06


def lengths_of(bucket):
    stride = max(1, TOK_MAX // (2 * BUCKETS))
    return TOK_MAX - bucket * stride


def noise_level(tstep, length):
    frac = (tstep.astype(jnp.float32) + 1.0) / TSTEPS
    shift = 1.0 + 2.0 * length.astype(jnp.float32) / TOK_MAX
    return shift * frac / (1.0 + (shift - 1.0) * frac)


def body(patches, noise, bucket, tstep, dest, embed_weight, gain, proj_weight, cotangent):
    n_dp = lax.axis_size("dp")
    n_fsdp = lax.axis_size("fsdp")
    myself = lax.axis_index("dp")
    feats = patches.shape[-1]
    width = proj_weight.shape[1]
    total_rows = CAP * TOK_MAX
    length_all = lengths_of(bucket[:, 0])
    dest_col = dest[:, 0]
    source_ids = jnp.arange(n_dp, dtype=jnp.int32)
    my_len = jnp.sum(jnp.where(source_ids == myself, length_all, 0))
    level = noise_level(tstep[0, 0], my_len)
    rows = jnp.arange(TOK_MAX, dtype=jnp.int32)
    mixed = (1.0 - level) * patches[0, 0].astype(jnp.float32) + level * noise[0, 0].astype(
        jnp.float32
    )
    latent = jnp.where(rows[:, None] < my_len, mixed, 0.0).astype(jnp.bfloat16)
    same = dest_col[:, None] == dest_col[None, :]
    earlier = source_ids[None, :] < source_ids[:, None]
    slot = jnp.sum((same & earlier).astype(jnp.int32), axis=1)
    slot_ids = jnp.arange(CAP, dtype=jnp.int32)
    chosen = (dest_col[None, :] == myself) & (slot[None, :] == slot_ids[:, None])
    plen = jnp.sum(jnp.where(chosen, length_all[None, :], 0), axis=1)
    arrived = lax.all_gather(latent[None], "dp", axis=0, tiled=True)
    packed = jnp.dot(
        chosen.astype(jnp.bfloat16),
        arrived.reshape(n_dp, TOK_MAX * feats),
        preferred_element_type=jnp.float32,
    )
    packed = packed.astype(jnp.bfloat16).reshape(total_rows, feats)
    hidden = jnp.dot(packed, embed_weight, preferred_element_type=jnp.float32)
    centered_input = hidden - jnp.mean(hidden, axis=1, keepdims=True)
    inverse_deviation = lax.rsqrt(
        jnp.mean(centered_input * centered_input, axis=1, keepdims=True) + norm_eps
    )
    standardized_input = centered_input * inverse_deviation
    normed_rows = (standardized_input * gain).astype(jnp.bfloat16)
    valid = (rows[None, :] < plen[:, None]).reshape(total_rows, 1)
    cot = cotangent[0, 0].reshape(total_rows, width)
    masked = jnp.where(valid, cot, jnp.zeros_like(cot))
    full_weight = lax.all_gather(proj_weight, "fsdp", axis=0, tiled=True)
    output = jnp.dot(normed_rows, full_weight, preferred_element_type=jnp.float32)
    back = lax.dot_general(
        masked, full_weight, (((1,), (1,)), ((), ())), preferred_element_type=jnp.float32
    )
    input_gradient = back * gain
    hidden_gradient = (
        input_gradient
        - jnp.mean(input_gradient, axis=1, keepdims=True)
        - standardized_input * jnp.mean(input_gradient * standardized_input, axis=1, keepdims=True)
    ) * inverse_deviation
    hidden_gradient = hidden_gradient.astype(jnp.bfloat16)
    partial_value = lax.dot_general(
        packed, hidden_gradient, (((0,), (0,)), ((), ())), preferred_element_type=jnp.float32
    )
    total = lax.psum(partial_value, ("dp", "fsdp"))
    embed_grad = total * float(n_dp * n_fsdp * TOK_MAX) ** (-0.5)
    projected = output.astype(jnp.bfloat16).reshape(1, 1, CAP, TOK_MAX, width)
    return (projected, embed_grad)


def solution(mesh):
    placed = (
        P("dp", "fsdp", None, None),
        P("dp", "fsdp", None, None),
        P(None, "fsdp"),
        P("dp", "fsdp"),
        P(None, "fsdp"),
        P(),
        P(),
        P("fsdp", None),
        P("dp", "fsdp", None, None, None),
    )
    return jax.shard_map(
        body,
        mesh=mesh,
        in_specs=placed,
        out_specs=(P("dp", "fsdp", None, None, None), P()),
        check_vma=False,
    )
```

profile of v0, /device:TPU:0, one launch (start us, length us, event | category | flops | bytes accessed | tf_op | source)
XLA Modules:
  0.0 205.2 jit_solution(9802073919326458462)
XLA Ops:
  7.2 0.0 copy-start
  7.2 0.0 all-gather.2.cloned.1.call-start
  7.2 0.7 all-gather.2.cloned.1.call-update
  7.9 0.0 all-reduce.2.cloned.1.call-start
  8.0 1.3 fusion.7
  10.6 0.7 iota_compare_fusion.2
  11.3 0.8 fusion.4
  12.1 32.6 %all_gather.6 = bf16[8,192,64]{1,2,0:T(8,128)(2,1)S(1)} all-gather(bf16[1,192,64]{1,2,0:T(8,128)(2,1)S(1)} %fusion.4), channel_id=1, replica_groups=mesh['dp'=8,'fsdp'=4] {'dp'}, dimensions={0}, use_global_device_ids=true | all-gather | bytes 221184 | tf_op jit(solution)/shard_map/all_gather | solution.py:47
  44.6 0.2 copy.16
  44.9 0.4 reshape.138
  45.2 0.9 convert_reduce_fusion
  46.2 0.7 broadcast_compare_fusion
  46.8 0.2 convolution_convert_fusion
  47.0 0.1 reshape.139
  47.1 0.7 subtract_bitcast_fusion
  47.8 0.1 select_reduce_fusion
  47.9 0.1 iota_compare_fusion.1
  48.0 0.1 lt.52
  48.1 0.0 copy-done
  48.1 0.0 copy-start.3
  48.1 0.7 fusion.10
  48.8 0.0 copy-start.1
  48.8 0.0 copy-start.4
  48.9 1.9 copy-done.1
  50.7 0.5 multiply_reduce_fusion.1
  51.2 0.0 copy-done.3
  51.2 0.2 bitcast_select_fusion
  51.4 6.9 %all-gather.2.cloned.1.call-done = bf16[2432,1216]{1,0:T(8,128)(2,1)} async-done(((bf16[608,1216]{1,0:T(8,128)(2,1)}), bf16[2432,1216]{1,0:T(8,128)(2,1)}) %all-gather.2.cloned.1.call-update) | async-done | bytes 5914640 | tf_op jit(solution)/shard_map/all_gather | solution.py:64
  58.3 0.0 copy-done.4
  58.3 0.0 copy-start.2
  58.3 7.0 %fusion.9 = (f32[384]{0:T(512)S(1)}, f32[384]{0:T(512)S(1)}, f32[384,2432]{1,0:T(8,128)S(1)}) fusion(f32[384]{0:T(512)S(1)} %add_rsqrt_fusion, f32[384,2432]{1,0:T(8,128)} %copy-done.1, f32[384]{0:T(512)S(1)} %broadcast_multiply_fusion.3, f32[2432]{0:T(1024)S(1)} %copy-done.4, bf16[384,1216]{1,0:T(8,128)(2,1)S(1)} %bitcast_select_fusion, ...), kind=kOutput, calls=%fused_computation.33 | convolution fusion | flops 2276817920 | bytes 14335488 | tf_op jit(solution)/shard_map/dot_general | solution.py:66
  65.3 0.0 copy-done.2
  65.3 1.9 fusion.3
  67.3 0.0 all-reduce.2.cloned.1.call-update
  67.3 7.4 %convolution_convert_fusion.1 = bf16[384,1216]{0,1:T(8,128)(2,1)S(1)} fusion(bf16[2432,1216]{1,0:T(8,128)(2,1)} %all-gather.2.cloned.1.call-done, f32[384,2432]{1,0:T(8,128)} %copy-done.1, f32[2432]{0:T(1024)S(1)} %copy-done.4, f32[384]{0:T(512)S(1)} %add_rsqrt_fusion, f32[384]{0:T(512)S(1)} %broadcast_multiply_fusion.3), kind=kOutput, calls=%fused_computation.7 | convolution fusion | flops 2275418112 | bytes 10596864 | tf_op jit(solution)/shard_map/dot_general | solution.py:65
  74.7 1.6 copy.17
  76.3 120.1 %all-reduce.2.cloned.1.call-done = f32[64,2432]{1,0:T(8,128)} async-done(((f32[64,2432]{1,0:T(8,128)}), f32[64,2432]{1,0:T(8,128)}) %all-reduce.2.cloned.1.call-update) | async-done | bytes 622608 | tf_op jit(solution)/shard_map/psum | solution.py:79
  196.4 2.0 broadcast_multiply_fusion
  (3 shorter events, 0.0 us)
Async XLA Ops:
  7.2 40.9 %copy-start = (bf16[64,2432]{1,0:T(8,128)(2,1)S(1)}, bf16[64,2432]{1,0:T(8,128)(2,1)}, u32[]{:S(2)}) copy-start(bf16[64,2432]{1,0:T(8,128)(2,1)} %param.14) | copy-start | bytes 933892
  7.2 51.1 %all-gather.2.cloned.1.call-start = ((), (), s32[]{:S(2)}) async-start(), calls=%async_computation | async-start | bytes 7782400 | tf_op jit(solution)/shard_map/all_gather | solution.py:64
  7.9 188.5 %all-reduce.2.cloned.1.call-start = ((), (), s32[]{:S(2)}) async-start(), calls=%async_computation.1 | async-start | bytes 1245184 | tf_op jit(solution)/shard_map/psum | solution.py:79
  48.1 3.1 %copy-start.3 = (bf16[1,1,2,192,1216]{4,3,2,1,0:T(8,128)(2,1)S(1)}, bf16[1,1,2,192,1216]{4,3,2,1,0:T(8,128)(2,1)}, u32[]{:S(2)}) copy-start(bf16[1,1,2,192,1216]{4,3,2,1,0:T(8,128)(2,1)} %param.17) | copy-start | bytes 2801668
  48.8 1.9 copy-start.1
  48.8 9.5 %copy-start.4 = (f32[2432]{0:T(1024)S(1)}, f32[2432]{0:T(1024)}, u32[]{:S(2)}) copy-start(f32[2432]{0:T(1024)} %param.15) | copy-start | bytes 29188
  58.3 7.0 %copy-start.2 = (f32[384,2432]{1,0:T(8,128)S(1)}, f32[384,2432]{1,0:T(8,128)}, u32[]{:S(2)}) copy-start(f32[384,2432]{1,0:T(8,128)} %copy-done.1) | copy-start | bytes 11206660
Sparse Core Ops, SparseCore 0:
  9.5 48.6 all-gather.1
  67.4 128.9 all-reduce.1
where the time goes:
time: 205 us
  waiting for transfers between devices  128 us (62%)
  blocking collectives  32.6 us (16%)
  matrix products  17.3 us (8%)
  between operations  15.5 us (8%)
  other arithmetic  7.85 us (4%)
  local copies, waits for them, and re-layouts  4.31 us (2%)
    psum x1, waiting for transfers between devices, body(): total = lax.psum(partial_value, ('dp', 'fsdp'))  120 us
    all_gather x1, blocking collectives, body(): arrived = lax.all_gather(latent[None], 'dp', axis=0, tiled=True)  32.6 us
    dot_general x1, matrix products, body(): jnp.dot(normed_rows, full_weight, preferred_element_type=jnp.float32)  7.39 us
    dot_general x1, matrix products, body(): lax.dot_general(masked, full_weight, (((1,), (1,)), ((), ())), preferred_...  7.03 us
    all_gather x1, waiting for transfers between devices, body(): full_weight = lax.all_gather(proj_weight, 'fsdp', axis=0, tiled=True)  6.86 us
  transfers between devices with their start and end apart: 2, of which 2 were waited for; matrix products, arithmetic and copies ran while one was open for 8% of the time, Pallas kernels for 0%

commit v1 on v0

--- a/solution.py
+++ b/solution.py
@@ -44,7 +44,9 @@
     slot_ids = jnp.arange(CAP, dtype=jnp.int32)
     chosen = (dest_col[None, :] == myself) & (slot[None, :] == slot_ids[:, None])
     plen = jnp.sum(jnp.where(chosen, length_all[None, :], 0), axis=1)
-    arrived = lax.all_gather(latent[None], "dp", axis=0, tiled=True)
+    block = latent[None]
+    stack = jnp.stack([block] * lax.axis_size("dp"))
+    arrived = jnp.concatenate(lax.all_to_all(stack, "dp", 0, 0), axis=0)
     packed = jnp.dot(
         chosen.astype(jnp.bfloat16),
         arrived.reshape(n_dp, TOK_MAX * feats),

time: 205 us -> 206 us (level)
  blocking collectives: 32.6 us -> 0 us
  waiting for transfers between devices: 128 us -> 151 us
  starting transfers between devices: 0.08 us -> 7.36 us
    all_gather x1 -> x0, blocking collectives: 32.6 us -> none  [body(): arrived = lax.all_gather(latent[None], 'dp', axis=0, tiled=True)]
    all_gather x1, waiting for transfers between devices: 6.86 us -> 25.3 us  [body(): full_weight = lax.all_gather(proj_weight, 'fsdp', axis=0, tiled=True)]
    all_to_all x0 -> x1, starting transfers between devices: none -> 7.28 us  [body(): arrived = jnp.concatenate(lax.all_to_all(stack, 'dp', 0, 0), axis=0)]
    all_to_all x0 -> x1, waiting for transfers between devices: none -> 4.91 us  [body(): arrived = jnp.concatenate(lax.all_to_all(stack, 'dp', 0, 0), axis=0)]
  transfers between devices with their start and end apart: 2 -> 3, of which waited for: 2 -> 3; matrix products, arithmetic and copies ran while one was open for 8% -> 9% of each run, Pallas kernels for 0% -> 0%
where the time goes in v1:
time: 206 us; the launch traced here: 205 us
  waiting for transfers between devices  151 us (73%)
  matrix products  17.3 us (8%)
  between operations  15.5 us (8%)
  other arithmetic  9.09 us (4%)
  starting transfers between devices  7.36 us (4%)
  local copies, waits for them, and re-layouts  5.02 us (2%)
    psum x1, waiting for transfers between devices, body(): total = lax.psum(partial_value, ('dp', 'fsdp'))  120 us
    all_gather x1, waiting for transfers between devices, body(): full_weight = lax.all_gather(proj_weight, 'fsdp', axis=0, tiled=True)  25.3 us
    dot_general x1, matrix products, body(): jnp.dot(normed_rows, full_weight, preferred_element_type=jnp.float32)  7.38 us
    all_to_all x1, starting transfers between devices, body(): arrived = jnp.concatenate(lax.all_to_all(stack, 'dp', 0, 0), axis=0)  7.28 us
    dot_general x1, matrix products, body(): lax.dot_general(masked, full_weight, (((1,), (1,)), ((), ())), preferred_...  7.04 us
    all_to_all x1, waiting for transfers between devices, body(): arrived = jnp.concatenate(lax.all_to_all(stack, 'dp', 0, 0), axis=0)  4.91 us
  transfers between devices with their start and end apart: 3, of which 3 were waited for; matrix products, arithmetic and copies ran while one was open for 9% of the time, Pallas kernels for 0%

profile of v1, /device:TPU:0, one launch (start us, length us, event | category | flops | bytes accessed | tf_op | source)
XLA Modules:
  0.0 205.2 jit_solution(17258590425931834537)
XLA Ops:
  7.2 0.0 copy-start
  7.2 0.0 all-gather.2.cloned.1.call-start
  7.2 0.7 all-gather.2.cloned.1.call-update
  7.9 1.3 fusion.7
  10.6 0.7 iota_compare_fusion.2
  11.2 0.8 fusion.4
  12.0 0.7 stack.3
  12.7 7.3 %all-to-all-start = ((bf16[8,1,192,64]{2,3,1,0:T(8,128)(2,1)}), bf16[8,1,192,64]{2,3,1,0:T(8,128)(2,1)S(1)}, u32[]{:S(2)}, u32[]{:S(2)}) async-start(bf16[8,1,192,64]{2,3,1,0:T(8,128)(2,1)} %stack.3), calls=%async_computation | async-start | bytes 524288 | tf_op jit(solution)/shard_map/all_to_all | solution.py:49
  20.0 0.0 all-reduce.2.cloned.1.call-start
  20.1 0.9 convert_reduce_fusion
  21.0 0.7 broadcast_compare_fusion
  21.6 0.7 subtract_bitcast_fusion
  22.3 0.1 select_reduce_fusion
  22.4 0.1 iota_compare_fusion.1
  22.5 0.1 lt.52
  22.6 1.4 bitcast_select_fusion
  24.0 4.9 %all-to-all-done = bf16[8,1,192,64]{2,3,1,0:T(8,128)(2,1)S(1)} async-done(((bf16[8,1,192,64]{2,3,1,0:T(8,128)(2,1)}), bf16[8,1,192,64]{2,3,1,0:T(8,128)(2,1)S(1)}, u32[]{:S(2)}, u32[]{:S(2)}) %all-to-all-start) | async-done | bytes 196640 | tf_op jit(solution)/shard_map/all_to_all | solution.py:49
  28.9 0.2 copy.17
  29.2 0.4 reshape_reshape.3
  29.5 0.2 convolution_convert_fusion
  29.7 0.1 reshape.84
  29.9 0.0 copy-done
  29.9 0.0 copy-start.3
  29.9 0.7 fusion.10
  30.6 0.0 copy-start.1
  30.6 1.9 copy-done.1
  32.5 0.5 multiply_reduce_fusion.1
  33.0 25.3 %all-gather.2.cloned.1.call-done = bf16[2432,1216]{1,0:T(8,128)(2,1)} async-done(((bf16[608,1216]{1,0:T(8,128)(2,1)}), bf16[2432,1216]{1,0:T(8,128)(2,1)}) %all-gather.2.cloned.1.call-update) | async-done | bytes 5914640 | tf_op jit(solution)/shard_map/all_gather | solution.py:66
  58.3 0.0 copy-done.3
  58.3 0.0 copy-start.2
  58.3 7.0 %fusion.9 = (f32[384]{0:T(512)S(1)}, f32[384]{0:T(512)S(1)}, f32[384,2432]{1,0:T(8,128)S(1)}) fusion(f32[384]{0:T(512)S(1)} %add_rsqrt_fusion, f32[384,2432]{1,0:T(8,128)} %copy-done.1, f32[384]{0:T(512)S(1)} %broadcast_multiply_fusion.3, f32[2432]{0:T(1024)S(1)} %copy-done.3, bf16[384,1216]{1,0:T(8,128)(2,1)S(1)} %bitcast_select_fusion, ...), kind=kOutput, calls=%fused_computation.33 | convolution fusion | flops 2276817920 | bytes 14335488 | tf_op jit(solution)/shard_map/dot_general | solution.py:68
  65.4 0.0 copy-done.2
  65.4 1.9 fusion.3
  67.3 0.0 all-reduce.2.cloned.1.call-update
  67.3 7.4 %convolution_convert_fusion.1 = bf16[384,1216]{0,1:T(8,128)(2,1)S(1)} fusion(bf16[2432,1216]{1,0:T(8,128)(2,1)} %all-gather.2.cloned.1.call-done, f32[384,2432]{1,0:T(8,128)} %copy-done.1, f32[2432]{0:T(1024)S(1)} %copy-done.3, f32[384]{0:T(512)S(1)} %add_rsqrt_fusion, f32[384]{0:T(512)S(1)} %broadcast_multiply_fusion.3), kind=kOutput, calls=%fused_computation.7 | convolution fusion | flops 2275418112 | bytes 10596864 | tf_op jit(solution)/shard_map/dot_general | solution.py:67
  74.7 1.6 copy.18
  76.3 120.0 %all-reduce.2.cloned.1.call-done = f32[64,2432]{1,0:T(8,128)} async-done(((f32[64,2432]{1,0:T(8,128)}), f32[64,2432]{1,0:T(8,128)}) %all-reduce.2.cloned.1.call-update) | async-done | bytes 622608 | tf_op jit(solution)/shard_map/psum | solution.py:81
  196.4 2.0 broadcast_multiply_fusion
  (3 shorter events, 0.0 us)
Async XLA Ops:
  7.2 22.7 %copy-start = (bf16[64,2432]{1,0:T(8,128)(2,1)S(1)}, bf16[64,2432]{1,0:T(8,128)(2,1)}, u32[]{:S(2)}) copy-start(bf16[64,2432]{1,0:T(8,128)(2,1)} %param.14) | copy-start | bytes 933892
  7.2 51.1 %all-gather.2.cloned.1.call-start = ((), (), s32[]{:S(2)}) async-start(), calls=%async_computation.1 | async-start | bytes 7782400 | tf_op jit(solution)/shard_map/all_gather | solution.py:66
  12.7 16.2 %all-to-all-start = ((bf16[8,1,192,64]{2,3,1,0:T(8,128)(2,1)}), bf16[8,1,192,64]{2,3,1,0:T(8,128)(2,1)S(1)}, u32[]{:S(2)}, u32[]{:S(2)}) async-start(bf16[8,1,192,64]{2,3,1,0:T(8,128)(2,1)} %stack.3), calls=%async_computation | async-start | bytes 524288 | tf_op jit(solution)/shard_map/all_to_all | solution.py:49
  20.0 176.3 %all-reduce.2.cloned.1.call-start = ((), (), s32[]{:S(2)}) async-start(), calls=%async_computation.2 | async-start | bytes 1245184 | tf_op jit(solution)/shard_map/psum | solution.py:81
  29.9 28.4 %copy-start.3 = (f32[2432]{0:T(1024)S(1)}, f32[2432]{0:T(1024)}, u32[]{:S(2)}) copy-start(f32[2432]{0:T(1024)} %param.15) | copy-start | bytes 29188
  30.6 1.9 copy-start.1
  58.3 7.1 %copy-start.2 = (f32[384,2432]{1,0:T(8,128)S(1)}, f32[384,2432]{1,0:T(8,128)}, u32[]{:S(2)}) copy-start(f32[384,2432]{1,0:T(8,128)} %copy-done.1) | copy-start | bytes 11206660
Sparse Core Ops, SparseCore 0:
  9.5 48.6 all-gather.1
  67.4 128.8 all-reduce.1

commit v2 on v0

--- a/solution.py
+++ b/solution.py
@@ -76,7 +76,7 @@
     partial_value = lax.dot_general(
         packed, hidden_gradient, (((0,), (0,)), ((), ())), preferred_element_type=jnp.float32
     )
-    total = lax.psum(partial_value, ("dp", "fsdp"))
+    total = lax.all_gather(partial_value, axis_name=("dp", "fsdp")).sum(axis=0)
     embed_grad = total * float(n_dp * n_fsdp * TOK_MAX) ** (-0.5)
     projected = output.astype(jnp.bfloat16).reshape(1, 1, CAP, TOK_MAX, width)
     return (projected, embed_grad)

time: 205 us -> 212 us (1.034)
  other arithmetic: 7.85 us -> 14.4 us
    psum x1 -> x0, waiting for transfers between devices: 120 us -> none  [body(): total = lax.psum(partial_value, ('dp', 'fsdp'))]
    all_gather x0 -> x1, waiting for transfers between devices: none -> 120 us  [body(): total = lax.all_gather(partial_value, axis_name=('dp', 'fsdp')).sum(axis=0)]
    reduce_sum x0 -> x1, other arithmetic: none -> 7.61 us  [body(): total = lax.all_gather(partial_value, axis_name=('dp', 'fsdp')).sum(axis=0)]
where the time goes in v2:
time: 212 us
  waiting for transfers between devices  128 us (60%)
  blocking collectives  32.6 us (15%)
  matrix products  17.3 us (8%)
  between operations  15.5 us (7%)
  other arithmetic  14.4 us (7%)
  local copies, waits for them, and re-layouts  4.26 us (2%)
    all_gather x1, waiting for transfers between devices, body(): total = lax.all_gather(partial_value, axis_name=('dp', 'fsdp')).sum(axis=0)  120 us
    all_gather x1, blocking collectives, body(): arrived = lax.all_gather(latent[None], 'dp', axis=0, tiled=True)  32.6 us
    reduce_sum x1, other arithmetic, body(): total = lax.all_gather(partial_value, axis_name=('dp', 'fsdp')).sum(axis=0)  7.61 us
    dot_general x1, matrix products, body(): jnp.dot(normed_rows, full_weight, preferred_element_type=jnp.float32)  7.39 us
    dot_general x1, matrix products, body(): lax.dot_general(masked, full_weight, (((1,), (1,)), ((), ())), preferred_...  7.03 us
    all_gather x1, waiting for transfers between devices, body(): full_weight = lax.all_gather(proj_weight, 'fsdp', axis=0, tiled=True)  6.9 us
  transfers between devices with their start and end apart: 2, of which 2 were waited for; matrix products, arithmetic and copies ran while one was open for 8% of the time, Pallas kernels for 0%

profile of v2, /device:TPU:0, one launch (start us, length us, event | category | flops | bytes accessed | tf_op | source)
XLA Modules:
  0.0 211.6 jit_solution(9415582434971725802)
XLA Ops:
  7.2 0.0 copy-start
  7.2 0.0 all-gather.4.cloned.1.call-start
  7.2 0.7 all-gather.4.cloned.1.call-update
  7.9 0.0 all-gather.6.cloned.1.call-start
  8.6 1.3 fusion.7
  10.6 0.9 convert_reduce_fusion
  11.5 0.7 broadcast_compare_fusion
  12.2 0.7 subtract_bitcast_fusion
  12.8 0.1 select_reduce_fusion
  13.0 0.1 iota_compare_fusion.1
  13.0 0.1 lt.52
  13.1 0.7 iota_compare_fusion.2
  13.8 0.8 fusion.4
  14.6 32.6 %all_gather.12 = bf16[8,192,64]{1,2,0:T(8,128)(2,1)S(1)} all-gather(bf16[1,192,64]{1,2,0:T(8,128)(2,1)S(1)} %fusion.4), channel_id=1, replica_groups=mesh['dp'=8,'fsdp'=4] {'dp'}, dimensions={0}, use_global_device_ids=true | all-gather | bytes 221184 | tf_op jit(solution)/shard_map/all_gather | solution.py:47
  47.1 0.2 copy.16
  47.4 0.4 reshape.138
  47.7 0.2 convolution_convert_fusion
  47.9 0.1 reshape.139
  48.1 0.0 copy-done
  48.1 0.0 copy-start.3
  48.1 0.7 fusion.10
  48.8 0.0 copy-start.1
  48.8 0.0 copy-start.4
  48.8 1.8 copy-done.1
  50.7 0.5 multiply_reduce_fusion.1
  51.2 0.0 copy-done.3
  51.2 0.2 bitcast_select_fusion
  51.4 6.9 %all-gather.4.cloned.1.call-done = bf16[2432,1216]{1,0:T(8,128)(2,1)} async-done(((bf16[608,1216]{1,0:T(8,128)(2,1)}), bf16[2432,1216]{1,0:T(8,128)(2,1)}) %all-gather.4.cloned.1.call-update) | async-done | bytes 5914640 | tf_op jit(solution)/shard_map/all_gather | solution.py:64
  58.3 0.0 copy-done.4
  58.3 0.0 copy-start.2
  58.3 7.0 %fusion.9 = (f32[384]{0:T(512)S(1)}, f32[384]{0:T(512)S(1)}, f32[384,2432]{1,0:T(8,128)S(1)}) fusion(f32[384]{0:T(512)S(1)} %add_rsqrt_fusion, f32[384,2432]{1,0:T(8,128)} %copy-done.1, f32[384]{0:T(512)S(1)} %broadcast_multiply_fusion.3, f32[2432]{0:T(1024)S(1)} %copy-done.4, bf16[384,1216]{1,0:T(8,128)(2,1)S(1)} %bitcast_select_fusion, ...), kind=kOutput, calls=%fused_computation.33 | convolution fusion | flops 2276817920 | bytes 14335488 | tf_op jit(solution)/shard_map/dot_general | solution.py:66
  65.3 0.0 copy-done.2
  65.4 1.9 fusion.3
  67.3 0.0 all-gather.6.cloned.1.call-update
  67.3 7.4 %convolution_convert_fusion.1 = bf16[384,1216]{0,1:T(8,128)(2,1)S(1)} fusion(bf16[2432,1216]{1,0:T(8,128)(2,1)} %all-gather.4.cloned.1.call-done, f32[384,2432]{1,0:T(8,128)} %copy-done.1, f32[2432]{0:T(1024)S(1)} %copy-done.4, f32[384]{0:T(512)S(1)} %add_rsqrt_fusion, f32[384]{0:T(512)S(1)} %broadcast_multiply_fusion.3), kind=kOutput, calls=%fused_computation.7 | convolution fusion | flops 2275418112 | bytes 10596864 | tf_op jit(solution)/shard_map/dot_general | solution.py:65
  74.7 1.6 copy.17
  76.3 120.0 %all-gather.6.cloned.1.call-done = f32[2048,2432]{1,0:T(8,128)} async-done(((f32[64,2432]{1,0:T(8,128)}), f32[2048,2432]{1,0:T(8,128)}) %all-gather.6.cloned.1.call-update) | async-done | bytes 19922960 | tf_op jit(solution)/shard_map/all_gather | solution.py:79
  196.3 7.6 %reduce_sum.79 = f32[64,2432]{1,0:T(8,128)S(1)} reduce(f32[32,64,2432]{2,1,0:T(8,128)} %bitcast.22, f32[]{:T(128)} %constant.37.clone.1), dimensions={0}, to_apply=%region_7.8 | reduce | flops 4825088 | bytes 20545540 | tf_op jit(solution)/shard_map/reduce_sum | solution.py:79
  203.9 0.9 broadcast_multiply_fusion
  (3 shorter events, 0.0 us)
Async XLA Ops:
  7.2 40.9 %copy-start = (bf16[64,2432]{1,0:T(8,128)(2,1)S(1)}, bf16[64,2432]{1,0:T(8,128)(2,1)}, u32[]{:S(2)}) copy-start(bf16[64,2432]{1,0:T(8,128)(2,1)} %param.14) | copy-start | bytes 933892
  7.2 51.1 %all-gather.4.cloned.1.call-start = ((), (), s32[]{:S(2)}) async-start(), calls=%async_computation | async-start | bytes 7782400 | tf_op jit(solution)/shard_map/all_gather | solution.py:64
  7.9 188.4 %all-gather.6.cloned.1.call-start = ((), (), s32[]{:S(2)}) async-start(), calls=%async_computation.1 | async-start | bytes 20545536 | tf_op jit(solution)/shard_map/all_gather | solution.py:79
  48.1 3.1 %copy-start.3 = (bf16[1,1,2,192,1216]{4,3,2,1,0:T(8,128)(2,1)S(1)}, bf16[1,1,2,192,1216]{4,3,2,1,0:T(8,128)(2,1)}, u32[]{:S(2)}) copy-start(bf16[1,1,2,192,1216]{4,3,2,1,0:T(8,128)(2,1)} %param.17) | copy-start | bytes 2801668
  48.8 1.9 copy-start.1
  48.8 9.5 %copy-start.4 = (f32[2432]{0:T(1024)S(1)}, f32[2432]{0:T(1024)}, u32[]{:S(2)}) copy-start(f32[2432]{0:T(1024)} %param.15) | copy-start | bytes 29188
  58.3 7.0 %copy-start.2 = (f32[384,2432]{1,0:T(8,128)S(1)}, f32[384,2432]{1,0:T(8,128)}, u32[]{:S(2)}) copy-start(f32[384,2432]{1,0:T(8,128)} %copy-done.1) | copy-start | bytes 11206660
Sparse Core Ops, SparseCore 0:
  9.5 48.6 all-gather.3
  67.4 128.8 all-gather.5
